TPU v7x, 32 devices: a whole 2x2x4 slice. The times are simulated.
32 devices in a mesh: rep: 4 (over z), fsdp: 8 (over y, x, core).
Axes of the slice: x: 2, y: 2, z: 4, core: 2. Of those that a mesh axis runs over, the one named last changes fastest.
Arguments:
- tokens: bfloat16 [16384, 2048], P(('rep', 'fsdp')), may hold values from -6 to 6
- norm_gain: float32 [2048], replicated, may hold values from 0.5 to 1.5
- outer_params: float32 [2, 2048, 4096], P(None, 'fsdp'), may hold values from -6 to 6
- momentum: float32 [2, 2048, 4096], P(None, 'fsdp'), may hold values from -6 to 6
- deltas: bfloat16 [4, 2, 2048, 4096], P('rep', None, 'fsdp'), may hold values from -6 to 6
Outputs:
- new_params: float32 [2, 2048, 4096], P(None, 'fsdp')
- new_momentum: float32 [2, 2048, 4096], P(None, 'fsdp')
- hidden: bfloat16 [16384, 4096], P(('rep', 'fsdp'))
All inputs are finite; a program needn't handle non-finite values.
Results may differ from a plain program's by a relative error of at most 0.01.
Values may be sent and summed in bfloat16 or wider, within the bound.
A program may use at most 192 MiB of HBM per device.

v0:
```python
import math
import jax
import jax.numpy as jnp
from jax import lax
from jax.sharding import PartitionSpec as P

EPS = 1e-05
MU = 0.9
RATE = 0.7


def advance(params, moment, summed, groups):
    outer_grad = summed * (1.0 / groups)
    moment_next = MU * moment + outer_grad
    params_next = params - RATE * (outer_grad + MU * moment_next)
    return (params_next, moment_next)


def body(tokens, norm_gain, outer_params, momentum, deltas):
    groups = lax.axis_size("rep")
    own_delta = deltas[0].astype(jnp.float32)
    summed = lax.psum(own_delta.astype(jnp.bfloat16), "rep").astype(jnp.float32)
    new_params, new_momentum = advance(outer_params, momentum, summed, groups)
    weights = new_params.astype(jnp.bfloat16)
    values = tokens.astype(jnp.float32)
    scale_rows = lax.rsqrt(jnp.mean(values * values, axis=-1, keepdims=True) + EPS)
    normed = (values * scale_rows * norm_gain).astype(jnp.bfloat16)
    factor = 1.0 / math.sqrt(normed.shape[1])
    results = []
    for which in range(2):
        results.append(
            jnp.dot(
                normed,
                lax.all_gather(weights[which], "fsdp", axis=0, tiled=True),
                preferred_element_type=jnp.float32,
            )
        )
    gate, up = (results[0], results[1])
    hidden = (jax.nn.silu(gate * factor) * (up * factor)).astype(jnp.bfloat16)
    return (new_params, new_momentum, hidden)


def solution(mesh):
    in_specs = (
        P(("rep", "fsdp"), None),
        P(),
        P(None, "fsdp", None),
        P(None, "fsdp", None),
        P("rep", None, "fsdp", None),
    )
    out_specs = (P(None, "fsdp", None), P(None, "fsdp", None), P(("rep", "fsdp"), None))
    return jax.shard_map(body, mesh=mesh, in_specs=in_specs, out_specs=out_specs, check_vma=False)
```

profile of v0, /device:TPU:0, one launch (start us, length us, event | category | flops | bytes accessed | tf_op | source)
XLA Modules:
  0.0 390.7 jit_solution(17987212437413564745)
XLA Ops:
  7.2 0.0 all-reduce.2.cloned.1.call-start
  7.2 0.7 all-reduce.2.cloned.1.call-update
  7.9 0.0 all-gather.7.cloned.1.call-start
  7.9 160.1 %all-reduce.2.cloned.1.call-done = bf16[2,256,4096]{2,1,0:T(8,128)(2,1)} async-done(((bf16[2,256,4096]{2,1,0:T(8,128)(2,1)}), bf16[2,256,4096]{2,1,0:T(8,128)(2,1)}) %all-reduce.2.cloned.1.call-update) | async-done | bytes 4194320 | tf_op jit(solution)/shard_map/psum | solution.py:22
  168.1 12.3 %fusion.11 = (bf16[2,256,4096]{2,1,0:T(8,128)(2,1)S(1)}, f32[2,256,4096]{2,1,0:T(8,128)}, f32[2,256,4096]{2,1,0:T(8,128)}) fusion(f32[2,256,4096]{2,1,0:T(8,128)} %param.7, bf16[2,256,4096]{2,1,0:T(8,128)(2,1)} %all-reduce.2.cloned.1.call-done, f32[2,256,4096]{2,1,0:T(8,128)} %param.8), kind=kLoop, calls=%fused_computation.14 | loop fusion | flops 18874368 | bytes 41943040 | tf_op jit(solution)/shard_map/convert_element_type | solution.py:24
  180.3 0.0 copy-start
  180.3 0.0 copy-start.1
  180.3 2.3 fusion.12
  182.6 0.0 all-gather.7.cloned.1.call-update
  182.7 0.0 all-gather.5.cloned.1.call-start
  182.7 0.7 all-gather.5.cloned.1.call-update
  183.4 0.0 copy-done
  183.4 0.5 fusion.6
  183.9 87.6 %all-gather.7.cloned.1.call-done = bf16[1,2048,4096]{2,1,0:T(8,128)(2,1)} async-done(((bf16[1,256,4096]{2,1,0:T(8,128)(2,1)}), bf16[1,2048,4096]{2,1,0:T(8,128)(2,1)}) %all-gather.7.cloned.1.call-update) | async-done | bytes 16777232 | tf_op jit(solution)/shard_map/all_gather | solution.py:34
  271.5 0.0 copy-done.1
  271.5 14.5 %fusion = f32[512,4096]{1,0:T(8,128)} fusion(bf16[1,2048,4096]{2,1,0:T(8,128)(2,1)} %all-gather.7.cloned.1.call-done, bf16[512,2048]{1,0:T(8,128)(2,1)S(1)} %copy-done, f32[2048]{0:T(1024)S(1)} %copy-done.1, f32[512]{0:T(512)S(1)} %add_rsqrt_fusion), kind=kOutput, calls=%fused_computation | convolution fusion | flops 8594128896 | bytes 27273216 | tf_op jit(solution)/shard_map/dot_general | solution.py:32
  286.0 77.7 %all-gather.5.cloned.1.call-done = bf16[1,2048,4096]{2,1,0:T(8,128)(2,1)} async-done(((bf16[1,256,4096]{2,1,0:T(8,128)(2,1)}), bf16[1,2048,4096]{2,1,0:T(8,128)(2,1)}) %all-gather.5.cloned.1.call-update) | async-done | bytes 16777232 | tf_op jit(solution)/shard_map/all_gather | solution.py:34
  363.7 20.5 %multiply_convert_fusion = bf16[512,4096]{1,0:T(8,128)(2,1)} fusion(f32[512,4096]{1,0:T(8,128)} %fusion, bf16[1,2048,4096]{2,1,0:T(8,128)(2,1)} %all-gather.5.cloned.1.call-done, bf16[512,2048]{1,0:T(8,128)(2,1)S(1)} %copy-done, f32[2048]{0:T(1024)S(1)} %copy-done.1, f32[512]{0:T(512)S(1)} %add_rsqrt_fusion), kind=kOutput, calls=%fused_computation.4 | convolution fusion | flops 8610906112 | bytes 31467520 | tf_op jit(solution)/shard_map/dot_general | solution.py:32
  (1 shorter events, 0.0 us)
Async XLA Ops:
  7.2 160.9 %all-reduce.2.cloned.1.call-start = ((), (), s32[]{:S(2)}) async-start(), calls=%async_computation | async-start | bytes 8388608 | tf_op jit(solution)/shard_map/psum | solution.py:22
  7.9 263.6 %all-gather.7.cloned.1.call-start = ((), (), s32[]{:S(2)}) async-start(), calls=%async_computation.2 | async-start | bytes 18874368 | tf_op jit(solution)/shard_map/all_gather | solution.py:34
  180.3 3.1 copy-start
  180.3 91.2 %copy-start.1 = (f32[2048]{0:T(1024)S(1)}, f32[2048]{0:T(1024)}, u32[]{:S(2)}) copy-start(f32[2048]{0:T(1024)} %param.6) | copy-start | bytes 24580
  182.7 181.1 %all-gather.5.cloned.1.call-start = ((), (), s32[]{:S(2)}) async-start(), calls=%async_computation.1 | async-start | bytes 18874368 | tf_op jit(solution)/shard_map/all_gather | solution.py:34
Sparse Core Ops, SparseCore 0:
  10.3 157.6 all-reduce.1
  182.8 88.6 all-gather.6
  274.0 89.7 all-gather.4
where the time goes:
time: 391 us
  waiting for transfers between devices  327 us (84%)
  matrix products  35 us (9%)
  between operations  13.8 us (4%)
  other arithmetic  12.8 us (3%)
    all_gather x2, waiting for transfers between devices, body(): lax.all_gather(weights[which], 'fsdp', axis=0, tiled=True)  165 us
    psum x1, waiting for transfers between devices, body(): summed = lax.psum(own_delta.astype(jnp.bfloat16), 'rep').astype(jnp.float32)  160 us
    dot_general x2, matrix products, body(): jnp.dot(normed, lax.all_gather(weights[which], 'fsdp', axis=0, tiled=True...  35 us
    convert_element_type x1, other arithmetic, body(): weights = new_params.astype(jnp.bfloat16)  12.3 us
  transfers between devices with their start and end apart: 3, of which 3 were waited for; matrix products, arithmetic and copies ran while one was open for 4% of the time, Pallas kernels for 0%

commit v1 on v0

--- a/solution.py
+++ b/solution.py
@@ -19,7 +19,9 @@
 def body(tokens, norm_gain, outer_params, momentum, deltas):
     groups = lax.axis_size("rep")
     own_delta = deltas[0].astype(jnp.float32)
-    summed = lax.psum(own_delta.astype(jnp.bfloat16), "rep").astype(jnp.float32)
+    summed = jnp.sum(lax.all_gather(own_delta.astype(jnp.bfloat16), "rep"), axis=0).astype(
+        jnp.float32
+    )
     new_params, new_momentum = advance(outer_params, momentum, summed, groups)
     weights = new_params.astype(jnp.bfloat16)
     values = tokens.astype(jnp.float32)

time: 391 us -> 533 us (1.36)
  waiting for transfers between devices: 327 us -> 457 us
  other arithmetic: 12.8 us -> 24.7 us
    all_gather x0 -> x1, waiting for transfers between devices: none -> 291 us  [body(): lax.all_gather(own_delta.astype(jnp.bfloat16), 'rep')]
    psum x1 -> x0, waiting for transfers between devices: 160 us -> none  [body(): summed = lax.psum(own_delta.astype(jnp.bfloat16), 'rep').astype(jnp.float32)]
    reduce_sum x0 -> x1, other arithmetic: none -> 11.9 us  [body(): jnp.sum(lax.all_gather(own_delta.astype(jnp.bfloat16), 'rep'), axis=0)]
  transfers between devices with their start and end apart: 3 -> 3, of which waited for: 3 -> 3; matrix products, arithmetic and copies ran while one was open for 4% -> 3% of each run, Pallas kernels for 0% -> 0%
where the time goes in v1:
time: 533 us
  waiting for transfers between devices  457 us (86%)
  matrix products  35 us (7%)
  other arithmetic  24.7 us (5%)
  between operations  13.8 us (3%)
    all_gather x1, waiting for transfers between devices, body(): lax.all_gather(own_delta.astype(jnp.bfloat16), 'rep')  291 us
    all_gather x2, waiting for transfers between devices, body(): lax.all_gather(weights[which], 'fsdp', axis=0, tiled=True)  165 us
    dot_general x2, matrix products, body(): jnp.dot(normed, lax.all_gather(weights[which], 'fsdp', axis=0, tiled=True...  35 us
    convert_element_type x1, other arithmetic, body(): weights = new_params.astype(jnp.bfloat16)  12.3 us
    reduce_sum x1, other arithmetic, body(): jnp.sum(lax.all_gather(own_delta.astype(jnp.bfloat16), 'rep'), axis=0)  11.9 us
  transfers between devices with their start and end apart: 3, of which 3 were waited for; matrix products, arithmetic and copies ran while one was open for 3% of the time, Pallas kernels for 0%

profile of v1, /device:TPU:0, one launch (start us, length us, event | category | flops | bytes accessed | tf_op | source)
XLA Modules:
  0.0 532.8 jit_solution(6178211435662958729)
XLA Ops:
  7.2 0.0 all-gather.6.cloned.1.call-start
  7.2 0.7 all-gather.6.cloned.1.call-update
  7.9 0.0 all-gather.10.cloned.1.call-start
  7.9 291.1 %all-gather.6.cloned.1.call-done = bf16[4,2,256,4096]{3,2,1,0:T(8,128)(2,1)} async-done(((bf16[1,2,256,4096]{3,2,1,0:T(8,128)(2,1)}), bf16[4,2,256,4096]{3,2,1,0:T(8,128)(2,1)}) %all-gather.6.cloned.1.call-update) | async-done | bytes 16777232 | tf_op jit(solution)/shard_map/all_gather | solution.py:22
  299.1 11.9 %reduce_sum.21 = bf16[2,256,4096]{2,1,0:T(8,128)(2,1)} reduce(bf16[4,2,256,4096]{3,2,1,0:T(8,128)(2,1)} %all-gather.6.cloned.1.call-done, bf16[]{:T(256)} %constant.3.clone.1), dimensions={0}, to_apply=%region_0.0 | reduce | flops 6291456 | bytes 20971522 | tf_op jit(solution)/shard_map/reduce_sum | solution.py:22
  310.9 12.3 %fusion.11 = (bf16[2,256,4096]{2,1,0:T(8,128)(2,1)S(1)}, f32[2,256,4096]{2,1,0:T(8,128)}, f32[2,256,4096]{2,1,0:T(8,128)}) fusion(f32[2,256,4096]{2,1,0:T(8,128)} %param.7, bf16[2,256,4096]{2,1,0:T(8,128)(2,1)} %reduce_sum.21, f32[2,256,4096]{2,1,0:T(8,128)} %param.8), kind=kLoop, calls=%fused_computation.14 | loop fusion | flops 18874368 | bytes 41943040 | tf_op jit(solution)/shard_map/convert_element_type | solution.py:26
  323.2 0.0 copy-start
  323.2 0.0 copy-start.1
  323.2 2.3 fusion.12
  325.5 0.0 all-gather.10.cloned.1.call-update
  325.5 0.0 all-gather.8.cloned.1.call-start
  325.6 0.7 all-gather.8.cloned.1.call-update
  326.3 0.0 copy-done
  326.3 0.5 fusion.6
  326.8 86.8 %all-gather.10.cloned.1.call-done = bf16[1,2048,4096]{2,1,0:T(8,128)(2,1)} async-done(((bf16[1,256,4096]{2,1,0:T(8,128)(2,1)}), bf16[1,2048,4096]{2,1,0:T(8,128)(2,1)}) %all-gather.10.cloned.1.call-update) | async-done | bytes 16777232 | tf_op jit(solution)/shard_map/all_gather | solution.py:36
  413.6 0.0 copy-done.1
  413.6 14.5 %fusion = f32[512,4096]{1,0:T(8,128)} fusion(bf16[1,2048,4096]{2,1,0:T(8,128)(2,1)} %all-gather.10.cloned.1.call-done, bf16[512,2048]{1,0:T(8,128)(2,1)S(1)} %copy-done, f32[2048]{0:T(1024)S(1)} %copy-done.1, f32[512]{0:T(512)S(1)} %add_rsqrt_fusion), kind=kOutput, calls=%fused_computation | convolution fusion | flops 8594128896 | bytes 27273216 | tf_op jit(solution)/shard_map/dot_general | solution.py:34
  428.1 77.7 %all-gather.8.cloned.1.call-done = bf16[1,2048,4096]{2,1,0:T(8,128)(2,1)} async-done(((bf16[1,256,4096]{2,1,0:T(8,128)(2,1)}), bf16[1,2048,4096]{2,1,0:T(8,128)(2,1)}) %all-gather.8.cloned.1.call-update) | async-done | bytes 16777232 | tf_op jit(solution)/shard_map/all_gather | solution.py:36
  505.8 20.5 %multiply_convert_fusion = bf16[512,4096]{1,0:T(8,128)(2,1)} fusion(f32[512,4096]{1,0:T(8,128)} %fusion, bf16[1,2048,4096]{2,1,0:T(8,128)(2,1)} %all-gather.8.cloned.1.call-done, bf16[512,2048]{1,0:T(8,128)(2,1)S(1)} %copy-done, f32[2048]{0:T(1024)S(1)} %copy-done.1, f32[512]{0:T(512)S(1)} %add_rsqrt_fusion), kind=kOutput, calls=%fused_computation.4 | convolution fusion | flops 8610906112 | bytes 31467520 | tf_op jit(solution)/shard_map/dot_general | solution.py:34
  (1 shorter events, 0.0 us)
Async XLA Ops:
  7.2 291.9 %all-gather.6.cloned.1.call-start = ((), (), s32[]{:S(2)}) async-start(), calls=%async_computation | async-start | bytes 20971520 | tf_op jit(solution)/shard_map/all_gather | solution.py:22
  7.9 405.7 %all-gather.10.cloned.1.call-start = ((), (), s32[]{:S(2)}) async-start(), calls=%async_computation.2 | async-start | bytes 18874368 | tf_op jit(solution)/shard_map/all_gather | solution.py:36
  323.2 3.1 copy-start
  323.2 90.4 %copy-start.1 = (f32[2048]{0:T(1024)S(1)}, f32[2048]{0:T(1024)}, u32[]{:S(2)}) copy-start(f32[2048]{0:T(1024)} %param.6) | copy-start | bytes 24580
  325.5 180.3 %all-gather.8.cloned.1.call-start = ((), (), s32[]{:S(2)}) async-start(), calls=%async_computation.1 | async-start | bytes 18874368 | tf_op jit(solution)/shard_map/all_gather | solution.py:36
Sparse Core Ops, SparseCore 0:
  9.5 289.4 all-gather.5
  325.7 87.9 all-gather.9
  416.1 89.7 all-gather.7
